TPU v7x, 32 devices: a whole 2x2x4 slice. The times are simulated.
32 devices in a mesh: gx: 2 (over x), gy: 4 (over z), gz: 4 (over y, core).
Axes of the slice: x: 2, y: 2, z: 4, core: 2. Of those that a mesh axis runs over, the one named last changes fastest.
Arguments:
- density: float32 [32, 64, 512], P('gx', 'gy', 'gz'), may hold values from 0.005 to 0.6, as said below
- coupling: float32 [14, 14], replicated, may hold values from -0.3 to 1.5, as said below
Outputs:
- potentials: float32 [14, 32, 64, 512], P(None, 'gx', 'gy', 'gz')
Inputs may be any that keep to these rules, and one draw needn't show every extreme that they name: Positive density. `coupling`: symmetric.
All inputs are finite; a program needn't handle non-finite values.
Results may differ from a plain program's by a relative error of at most 0.0003.
Values sent between devices are 32-bit elements; how exact they have to be, the bound alone decides.
A program may use at most 128 MiB of HBM per device.

v0:
```python
import math
import jax
import jax.numpy as jnp
from jax import lax
from jax.sharding import PartitionSpec as P

zab_ratio = 0.8491 / 9.0
q_cut = 5.0
mesh_step = 0.07
range_factor = 1.0
local_weight = 0.25
spline_root = math.sqrt(3.0) - 2.0
highest = lax.Precision.HIGHEST


def extended(cells, sides, width):
    for axis, dim in sides:
        count = lax.axis_size(axis)
        head = lax.slice_in_dim(cells, 0, width, axis=dim)
        tail = lax.slice_in_dim(cells, cells.shape[dim] - width, cells.shape[dim], axis=dim)
        cells = jnp.concatenate(
            [
                lax.ppermute(tail, axis, [(i, (i + 1) % count) for i in range(count)]),
                cells,
                lax.ppermute(head, axis, [((i + 1) % count, i) for i in range(count)]),
            ],
            axis=dim,
        )
    return cells


def interior(padded, dim_index, offset):
    picks = []
    for other in range(3):
        lowest = 2 + offset if other == dim_index else 2
        picks.append(slice(lowest, lowest + padded.shape[other] - 4))
    return padded[tuple(picks)]


def saturated_wavevector(density, grad_sq):
    fermi_k = jnp.cbrt(3.0 * math.pi * math.pi * density)
    reduced = grad_sq / (4.0 * fermi_k * fermi_k * density * density)
    raw_q = fermi_k * (1.0 + zab_ratio * reduced)
    scaled = raw_q / q_cut
    powered = scaled
    series = jnp.zeros_like(scaled)
    for term_order in range(1, 13):
        series = series + powered / term_order
        powered = powered * scaled
    return q_cut * (1.0 - jnp.exp(-series))


def spline_weights(q_zero, q_top, qpoints):
    position = jnp.maximum(qpoints - 1.0 + jnp.log(q_zero / q_top) / mesh_step, 0.0)
    knot_ids = jnp.arange(-1, qpoints + 1, dtype=jnp.int32)
    offset = jnp.abs(position[None, :] - knot_ids.astype(jnp.float32)[:, None])
    bspline = (
        jnp.maximum(2.0 - offset, 0.0) ** 3 - 4.0 * jnp.maximum(1.0 - offset, 0.0) ** 3
    ) / 6.0
    q_nodes = jnp.arange(qpoints, dtype=jnp.int32)
    distance = jnp.abs(knot_ids[:, None] - q_nodes[None, :])
    parity = (1 - 2 * (distance % 2)).astype(jnp.float32)
    matrix = (
        math.sqrt(3.0) * parity * jnp.exp(distance.astype(jnp.float32) * math.log(-spline_root))
    )
    return jnp.dot(matrix.T, bspline, precision=highest)


def build_thetas(dens_field, q_field, q_top, qpoints):
    weights = spline_weights(q_field.reshape(-1), q_top, qpoints)
    return (weights * dens_field.reshape(1, -1)).reshape((qpoints,) + dens_field.shape)


def join_planes(joined, count, slab_rows, groups_y, groups_z):
    size_y, size_z = (joined.shape[-2], joined.shape[-1])
    planes = joined.reshape(count, slab_rows, groups_y, groups_z, size_y, size_z)
    return planes.transpose(0, 1, 2, 4, 3, 5).reshape(
        count, slab_rows, groups_y * size_y, groups_z * size_z
    )


def wave_squared(wave_ids, length):
    folded = jnp.where(2 * wave_ids < length, wave_ids, wave_ids - length)
    wavenum = 2.0 * math.pi / length * folded.astype(jnp.float32)
    return wavenum * wavenum


def dft_tables(length):
    wave_ids = jnp.arange(length, dtype=jnp.int32)
    phases = wave_ids[:, None] * wave_ids[None, :] % length
    angles = 2.0 * math.pi / length * phases.astype(jnp.float32)
    return (jnp.cos(angles), jnp.sin(angles))


def complex_table(length, direction_sign):
    cosine, sines = dft_tables(length)
    top_row = jnp.stack([cosine, -direction_sign * sines], axis=1)
    bottom_row = jnp.stack([direction_sign * sines, cosine], axis=1)
    return jnp.stack([top_row, bottom_row], axis=0)


def forward_z(field_in):
    cosine, sines = dft_tables(field_in.shape[-1])
    matrix = jnp.stack([cosine, -sines], axis=1)
    return jnp.einsum("aryz,zpk->paryk", field_in, matrix, precision=highest)


def along_y(complex_pair, direction_sign):
    matrix = complex_table(complex_pair.shape[3], direction_sign)
    return jnp.einsum("pkqy,qaryz->parkz", matrix, complex_pair, precision=highest)


def along_x(complex_pair, direction_sign):
    matrix = complex_table(complex_pair.shape[2], direction_sign)
    return jnp.einsum("pkqx,qaxm->pakm", matrix, complex_pair, precision=highest)


def inverse_z(complex_pair):
    cosine, sines = dft_tables(complex_pair.shape[-1])
    matrix = jnp.stack([cosine, -sines], axis=0)
    return jnp.einsum("paryz,pzk->aryk", complex_pair, matrix, precision=highest)


def apply_kernel(spectra, k_squared, coupling, q_top):
    qpoints = coupling.shape[0]
    q_nodes = jnp.arange(qpoints, dtype=jnp.int32)
    q_mesh = q_top * jnp.exp(-mesh_step * (qpoints - 1 - q_nodes).astype(jnp.float32))
    masses = range_factor * q_mesh[:, None] * q_mesh[None, :]

    def add_source(source, summed):
        mass_col = lax.dynamic_index_in_dim(masses, source, 1, keepdims=False)[:, None, None]
        coupling_col = lax.dynamic_index_in_dim(coupling, source, 1, keepdims=False)[:, None, None]
        factor = coupling_col * (local_weight + mass_col / (k_squared[None] + mass_col))
        spectrum = lax.dynamic_index_in_dim(spectra, source, 1, keepdims=False)
        return summed + factor[None] * spectrum[:, None]

    return lax.fori_loop(0, qpoints, add_source, jnp.zeros_like(spectra))


def body(density, coupling):
    size_x, size_y, size_z = density.shape
    qpoints = coupling.shape[0]
    groups_x, groups_y, groups_z = (lax.axis_size("gx"), lax.axis_size("gy"), lax.axis_size("gz"))
    full_x, full_y, full_z = (size_x * groups_x, size_y * groups_y, size_z * groups_z)
    scale_inv = 1.0 / (full_x * full_y * full_z)
    padded = extended(density, (("gx", 0), ("gy", 1), ("gz", 2)), 2)
    grad_sq = jnp.zeros_like(density)
    for dim_index in range(3):
        nearer = interior(padded, dim_index, 1) - interior(padded, dim_index, -1)
        farther = interior(padded, dim_index, 2) - interior(padded, dim_index, -2)
        gradient = (8.0 * nearer - farther) / 12.0
        grad_sq = grad_sq + gradient * gradient
    q_zero = saturated_wavevector(density, grad_sq)
    q_top = lax.pmax(jnp.max(q_zero), ("gx", "gy", "gz"))
    x_waves = wave_squared(jnp.arange(full_x, dtype=jnp.int32), full_x)
    slab_rows = size_x // (groups_y * groups_z)
    thetas = build_thetas(density, q_zero, q_top, qpoints)
    joined = lax.all_to_all(
        thetas.reshape(qpoints, size_x, 1, size_y, size_z),
        ("gy", "gz"),
        split_axis=1,
        concat_axis=2,
        tiled=True,
    )
    planes = join_planes(joined, qpoints, slab_rows, groups_y, groups_z)
    spectra = along_y(forward_z(planes), -1.0)
    plane_part = full_y * full_z // (groups_x * groups_y * groups_z)
    xlines = lax.all_to_all(
        spectra.reshape(2, qpoints, slab_rows, full_y * full_z),
        ("gx", "gy", "gz"),
        split_axis=3,
        concat_axis=2,
        tiled=True,
    )
    flat_index = lax.axis_index(("gx", "gy", "gz")) * plane_part + jnp.arange(
        plane_part, dtype=jnp.int32
    )
    k_squared = (
        x_waves[:, None]
        + (wave_squared(flat_index // full_z, full_y) + wave_squared(flat_index % full_z, full_z))[
            None, :
        ]
    )
    products = along_x(apply_kernel(along_x(xlines, -1.0), k_squared, coupling, q_top), 1.0)
    returned = lax.all_to_all(
        products, ("gx", "gy", "gz"), split_axis=2, concat_axis=3, tiled=True
    ).reshape(2, qpoints, slab_rows, full_y, full_z)
    fields = inverse_z(along_y(returned, 1.0)) * scale_inv
    spread = fields.reshape(qpoints, slab_rows, groups_y, size_y, groups_z, size_z)
    spread = spread.transpose(0, 1, 2, 4, 3, 5).reshape(
        qpoints, slab_rows, groups_y * groups_z, size_y, size_z
    )
    blocks = lax.all_to_all(spread, ("gy", "gz"), split_axis=2, concat_axis=1, tiled=True)
    return blocks.reshape(qpoints, size_x, size_y, size_z)


def solution(mesh):
    placed = (P("gx", "gy", "gz"), P())
    return jax.shard_map(
        body, mesh=mesh, in_specs=placed, out_specs=P(None, "gx", "gy", "gz"), check_vma=False
    )
```

profile of v0, /device:TPU:1, one launch (start us, length us, event | category | flops | bytes accessed | tf_op | source)
XLA Modules:
  0.0 683.4 jit_solution(6947540007924352375)
XLA Ops:
  18.2 6.7 collective-permute-done.4
  26.1 36.2 %pmax.7 = f32[]{:T(128)} all-reduce(f32[]{:T(128)} %get-tuple-element.178), channel_id=1, replica_groups=mesh['gx'=2,'gy'=4,'gz'=4] {'gx','gy','gz'}, use_global_device_ids=true, to_apply=%region_1.0 | all-reduce | flops 1 | bytes 8 | tf_op jit(solution)/shard_map/pmax | solution.py:154
  67.5 7.5 %all-to-all-start = ((f32[14,16,1,16,128]{4,3,0,2,1:T(8,128)}), f32[14,16,1,16,128]{4,3,0,2,1:T(8,128)S(1)}, u32[]{:S(2)}, u32[]{:S(2)}) async-start(f32[14,16,1,16,128]{4,3,0,2,1:T(8,128)} %copy.18), calls=%async_computation | async-start | bytes 3670016 | tf_op jit(solution)/shard_map/all_to_all | solution.py:158
  75.3 5.3 sine_negate_fusion.1
  80.6 31.4 %all-to-all-done = f32[14,16,1,16,128]{4,3,0,2,1:T(8,128)S(1)} async-done(((f32[14,16,1,16,128]{4,3,0,2,1:T(8,128)}), f32[14,16,1,16,128]{4,3,0,2,1:T(8,128)S(1)}, u32[]{:S(2)}, u32[]{:S(2)}) %all-to-all-start) | async-done | bytes 1835040 | tf_op jit(solution)/shard_map/all_to_all | solution.py:158
  116.6 7.6 %fusion.28 = f32[2,14,64,512,1]{3,2,1,0,4:T(8,128)S(1)} fusion(f32[14,64,512,1]{2,1,0,3:T(8,128)S(1)} %reshape.462, f32[512,1,512]{2,0,1:T(8,128)S(1)} %get-tuple-element.209, f32[512,1,512]{2,0,1:T(8,128)} %get-tuple-element.210), kind=kOutput, calls=%fused_computation.36 | convolution fusion | flops 5637668864 | bytes 7602176 | tf_op jit(solution)/shard_map/aryz,zpk->paryk/dot_general | solution.py:105
  124.2 5.8 fusion.29
  130.0 26.4 %copy.41 = f32[2,14,1,64,512]{1,0,4,3,2:T(2,128)} copy(f32[2,14,1,64,512]{4,3,0,1,2:T(8,128)} %fusion.29) | data formatting | bytes 7340032 | tf_op jit(solution)/shard_map/reshape | solution.py:169
  156.4 56.7 %reshape.479 = f32[32,1,28672]{2,1,0:T(1,128)} reshape(f32[32768,1,2,14]{3,2,1,0:T(2,128)} %bitcast.123) | data formatting | bytes 7340032
  213.1 9.2 %all-to-all-start.1 = ((f32[32,1,28672]{2,1,0:T(1,128)}), f32[32,1,28672]{2,1,0:T(1,128)}, u32[]{:S(2)}, u32[]{:S(2)}) async-start(f32[32,1,28672]{2,1,0:T(1,128)} %reshape.479), calls=%async_computation.1 | async-start | bytes 7340032 | tf_op jit(solution)/shard_map/all_to_all | solution.py:168
  223.3 81.8 %all-to-all-done.1 = f32[32,1,28672]{2,1,0:T(1,128)} async-done(((f32[32,1,28672]{2,1,0:T(1,128)}), f32[32,1,28672]{2,1,0:T(1,128)}, u32[]{:S(2)}, u32[]{:S(2)}) %all-to-all-start.1) | async-done | bytes 3670048 | tf_op jit(solution)/shard_map/all_to_all | solution.py:168
  305.7 12.8 %reduce = f32[32,28672]{1,0:T(8,128)} reduce(f32[32,1,28672]{2,1,0:T(1,128)} %all-to-all-done.1, f32[]{:T(128)} %broadcast.803), dimensions={1}, to_apply=%all_to_all.11.reduce_sub_computation | reduce | bytes 7340036 | tf_op jit(solution)/shard_map/all_to_all | solution.py:168
  318.5 72.2 %reshape.480 = f32[32768,1,2,14]{3,2,1,0:T(2,128)} reshape(f32[32,28672]{1,0:T(8,128)} %reduce) | data formatting | bytes 7340032
  390.7 28.0 %copy.32 = f32[2,14,32,1024,1]{3,2,0,4,1:T(8,128)} copy(f32[2,14,32,1024,1]{1,0,3,2,4:T(2,128)} %bitcast.124) | data formatting | bytes 7340032 | tf_op jit(solution)/shard_map/all_to_all | solution.py:168
  418.7 6.4 convolution_bitcast_fusion
  425.2 85.2 %while.14 = (s32[]{:T(128)}, f32[2,14,32,1024]{3,2,1,0:T(8,128)}, f32[14,14]{0,1:T(8,128)S(1)}, f32[14,14]{0,1:T(8,128)S(1)}, f32[2,14,32,1024]{3,2,0,1:T(8,128)...) while((s32[]{:T(128)}, f32[2,14,32,1024]{3,2,1,0:T(8,128)}, ...), condition=%wide.region_3.4_spmd.clone, body=%wide.region_2.3_spmd.clone.sunk | while | flops 4620291 | bytes 12063295 | solution.py:137
  431.2 4.8 select_add_fusion.2
  437.4 4.8 select_add_fusion.2
  443.6 4.8 select_add_fusion.2
  449.8 4.8 select_add_fusion.2
  456.0 4.8 select_add_fusion.2
  462.2 4.8 select_add_fusion.2
  468.4 4.8 select_add_fusion.2
  474.6 4.8 select_add_fusion.2
  487.0 4.8 select_add_fusion.2
  510.4 6.6 fusion.32
  530.2 78.8 %all-to-all-done.2 = f32[2,14,32,1024]{3,0,1,2:T(2,128)} async-done(((f32[2,14,32,1024]{3,0,1,2:T(2,128)}), f32[2,14,32,1024]{3,0,1,2:T(2,128)}, u32[]{:S(2)}, u32[]{:S(2)}) %all-to-all-start.2) | async-done | bytes 3670048 | tf_op jit(solution)/shard_map/all_to_all | solution.py:185
  609.0 6.0 copy.26
  615.1 4.9 reshape.472
  620.0 6.0 fusion.6
  626.0 7.1 %bitcast_multiply_fusion = f32[14,64,512]{2,1,0:T(8,128)} fusion(f32[1,512,512]{2,1,0:T(8,128)S(1)} %get-tuple-element.215, f32[1,512,512]{2,1,0:T(8,128)S(1)} %get-tuple-element.216, f32[14,512,2,64,1]{1,3,4,2,0:T(8,128)S(1)} %fusion.6), kind=kOutput, calls=%fused_computation.40 | convolution fusion | flops 5638127616 | bytes 7602176 | tf_op jit(solution)/shard_map/paryz,pzk->aryk/dot_general | solution.py:121
  635.2 46.6 %all_to_all.19 = f32[14,1,16,16,128]{4,3,0,1,2:T(8,128)S(1)} all-to-all(f32[14,1,16,16,128]{4,3,0,1,2:T(8,128)S(1)} %bitcast.130), channel_id=1, replica_groups=mesh['gx'=2,'gy'=4,'gz'=4] {'gy','gz'}, dimensions={2} | all-to-all | bytes 3670016 | tf_op jit(solution)/shard_map/all_to_all | solution.py:193
  (111 shorter events, 89.4 us)
Async XLA Ops:
  0.0 24.9 %copy-start = (f32[16,16,128]{2,1,0:T(8,128)S(1)}, f32[16,16,128]{2,1,0:T(8,128)}, u32[]{:S(2)}) copy-start(f32[16,16,128]{2,1,0:T(8,128)} %param.4) | copy-start | bytes 393220
  0.8 3.2 collective-permute-start.1
  2.8 2.6 collective-permute-start
  5.4 4.6 collective-permute-start.2
  9.1 4.4 collective-permute-start.3
  13.7 11.2 %collective-permute-start.4 = (f32[20,20,2]{2,1,0:T(8,128)S(1)}, f32[20,20,2]{2,1,0:T(8,128)S(1)}, u32[]{:S(2)}, u32[]{:S(2)}) collective-permute-start(f32[20,20,2]{2,1,0:T(8,128)S(1)} %get-tuple-element.182), channel_id=1, source_target_pairs={{1,0},{2,1},{3,2},{0,3},{5,4},{6,5},{7,6},{4,7},{9,8},{10,9},{11,1... | collective-permute-start | bytes 9608 | tf_op jit(solution)/shard_map/ppermute | solution.py:25
  17.0 7.9 %collective-permute-start.5 = (f32[20,20,2]{2,1,0:T(8,128)S(1)}, f32[20,20,2]{2,1,0:T(8,128)S(1)}, u32[]{:S(2)}, u32[]{:S(2)}) collective-permute-start(f32[20,20,2]{2,1,0:T(8,128)S(1)} %get-tuple-element.183), channel_id=1, source_target_pairs={{0,1},{1,2},{2,3},{3,0},{4,5},{5,6},{6,7},{7,4},{8,9},{9,10},{10,1... | collective-permute-start | bytes 9608 | tf_op jit(solution)/shard_map/ppermute | solution.py:23
  67.5 44.4 %all-to-all-start = ((f32[14,16,1,16,128]{4,3,0,2,1:T(8,128)}), f32[14,16,1,16,128]{4,3,0,2,1:T(8,128)S(1)}, u32[]{:S(2)}, u32[]{:S(2)}) async-start(f32[14,16,1,16,128]{4,3,0,2,1:T(8,128)} %copy.18), calls=%async_computation | async-start | bytes 3670016 | tf_op jit(solution)/shard_map/all_to_all | solution.py:158
  213.1 9.2 %copy-start.1 = (f32[14,14]{1,0:T(8,128)S(1)}, f32[14,14]{1,0:T(8,128)}, u32[]{:S(2)}) copy-start(f32[14,14]{1,0:T(8,128)} %param.5) | copy-start | bytes 2356
  213.1 92.0 %all-to-all-start.1 = ((f32[32,1,28672]{2,1,0:T(1,128)}), f32[32,1,28672]{2,1,0:T(1,128)}, u32[]{:S(2)}, u32[]{:S(2)}) async-start(f32[32,1,28672]{2,1,0:T(1,128)} %reshape.479), calls=%async_computation.1 | async-start | bytes 7340032 | tf_op jit(solution)/shard_map/all_to_all | solution.py:168
  521.7 87.4 %all-to-all-start.2 = ((f32[2,14,32,1024]{3,0,1,2:T(2,128)}), f32[2,14,32,1024]{3,0,1,2:T(2,128)}, u32[]{:S(2)}, u32[]{:S(2)}) async-start(f32[2,14,32,1024]{3,0,1,2:T(2,128)} %copy.25), calls=%async_computation.2 | async-start | bytes 7340032 | tf_op jit(solution)/shard_map/all_to_all | solution.py:185
where the time goes:
time: 693 us; the launch traced here: 683 us
  local copies, waits for them, and re-layouts  225 us (32%)
  waiting for transfers between devices  205 us (30%)
  other arithmetic  96 us (14%)
  blocking collectives  82.7 us (12%)
  matrix products  42.2 us (6%)
  starting transfers between devices  31.3 us (5%)
    unnamed x11, local copies, waits for them, and re-layouts  130 us
    all_to_all x1, waiting for transfers between devices, body(): lax.all_to_all(spectra.reshape(2, qpoints, slab_rows, full_y * full_z), (...  81.8 us
    all_to_all x1, waiting for transfers between devices, body(): lax.all_to_all(products, ('gx', 'gy', 'gz'), split_axis=2, concat_axis=3,...  78.8 us
    add x14, other arithmetic, add_source(): return summed + factor[None] * spectrum[:, None]  64.5 us
    all_to_all x1, blocking collectives, body(): lax.all_to_all(spread, ('gy', 'gz'), split_axis=2, concat_axis=1, tiled=T...  46.6 us
    pmax x1, blocking collectives, body(): q_top = lax.pmax(jnp.max(q_zero), ('gx', 'gy', 'gz'))  36.2 us
    all_to_all x1, waiting for transfers between devices, body(): lax.all_to_all(thetas.reshape(qpoints, size_x, 1, size_y, size_z), ('gy',...  31.4 us
    all_to_all x2, local copies, waits for them, and re-layouts, body(): lax.all_to_all(spectra.reshape(2, qpoints, slab_rows, full_y * full_z), (...  28.6 us
  transfers between devices with their start and end apart: 9, of which 8 were waited for; matrix products, arithmetic and copies ran while one was open for 2% of the time, Pallas kernels for 0%

commit v1 on v0

--- a/solution.py
+++ b/solution.py
@@ -11,6 +11,13 @@
 local_weight = 0.25
 spline_root = math.sqrt(3.0) - 2.0
 highest = lax.Precision.HIGHEST
+
+
+def stacked_exchange(value, axis, split, join):
+    count = lax.axis_size(axis)
+    tiles = jnp.stack(jnp.split(value, count, axis=split), axis=0)
+    tiles = lax.all_to_all(tiles, axis, split_axis=0, concat_axis=0)
+    return jnp.concatenate(tiles, axis=join)
 
 
 def extended(cells, sides, width):
@@ -182,9 +189,9 @@
         ]
     )
     products = along_x(apply_kernel(along_x(xlines, -1.0), k_squared, coupling, q_top), 1.0)
-    returned = lax.all_to_all(
-        products, ("gx", "gy", "gz"), split_axis=2, concat_axis=3, tiled=True
-    ).reshape(2, qpoints, slab_rows, full_y, full_z)
+    returned = stacked_exchange(products, ("gx", "gy", "gz"), 2, 3).reshape(
+        2, qpoints, slab_rows, full_y, full_z
+    )
     fields = inverse_z(along_y(returned, 1.0)) * scale_inv
     spread = fields.reshape(qpoints, slab_rows, groups_y, size_y, groups_z, size_z)
     spread = spread.transpose(0, 1, 2, 4, 3, 5).reshape(

time: 693 us -> 716 us (1.033)
  local copies, waits for them, and re-layouts: 225 us -> 246 us
    unnamed x11 -> x42, local copies, waits for them, and re-layouts: 130 us -> 152 us
where the time goes in v1:
time: 716 us; the launch traced here: 706 us
  local copies, waits for them, and re-layouts  246 us (34%)
  waiting for transfers between devices  205 us (29%)
  other arithmetic  97.2 us (14%)
  blocking collectives  82.8 us (12%)
  matrix products  42.2 us (6%)
  starting transfers between devices  31.3 us (4%)
    unnamed x42, local copies, waits for them, and re-layouts  152 us
    all_to_all x1, waiting for transfers between devices, body(): lax.all_to_all(spectra.reshape(2, qpoints, slab_rows, full_y * full_z), (...  81.7 us
    all_to_all x1, waiting for transfers between devices, stacked_exchange(): tiles = lax.all_to_all(tiles, axis, split_axis=0, concat_axis=0)  78.8 us
    add x14, other arithmetic, add_source(): return summed + factor[None] * spectrum[:, None]  64.6 us
    all_to_all x1, blocking collectives, body(): lax.all_to_all(spread, ('gy', 'gz'), split_axis=2, concat_axis=1, tiled=T...  46.6 us
    pmax x1, blocking collectives, body(): q_top = lax.pmax(jnp.max(q_zero), ('gx', 'gy', 'gz'))  36.2 us
    all_to_all x1, waiting for transfers between devices, body(): lax.all_to_all(thetas.reshape(qpoints, size_x, 1, size_y, size_z), ('gy',...  31.4 us
    all_to_all x2, local copies, waits for them, and re-layouts, body(): lax.all_to_all(spectra.reshape(2, qpoints, slab_rows, full_y * full_z), (...  28.6 us
  transfers between devices with their start and end apart: 9, of which 8 were waited for; matrix products, arithmetic and copies ran while one was open for 2% of the time, Pallas kernels for 0%

profile of v1, /device:TPU:1, one launch (start us, length us, event | category | flops | bytes accessed | tf_op | source)
XLA Modules:
  0.0 705.9 jit_solution(17958896206293218751)
XLA Ops:
  18.2 6.7 collective-permute-done.4
  27.1 36.2 %pmax.7 = f32[]{:T(128)} all-reduce(f32[]{:T(128)} %get-tuple-element.185), channel_id=1, replica_groups=mesh['gx'=2,'gy'=4,'gz'=4] {'gx','gy','gz'}, use_global_device_ids=true, to_apply=%region_1.0 | all-reduce | flops 1 | bytes 8 | tf_op jit(solution)/shard_map/pmax | solution.py:161
  68.7 7.5 %all-to-all-start = ((f32[14,16,1,16,128]{4,3,0,2,1:T(8,128)}), f32[14,16,1,16,128]{4,3,0,2,1:T(8,128)S(1)}, u32[]{:S(2)}, u32[]{:S(2)}) async-start(f32[14,16,1,16,128]{4,3,0,2,1:T(8,128)} %copy.119), calls=%async_computation | async-start | bytes 3670016 | tf_op jit(solution)/shard_map/all_to_all | solution.py:165
  76.5 5.3 sine_negate_fusion.1
  81.8 31.4 %all-to-all-done = f32[14,16,1,16,128]{4,3,0,2,1:T(8,128)S(1)} async-done(((f32[14,16,1,16,128]{4,3,0,2,1:T(8,128)}), f32[14,16,1,16,128]{4,3,0,2,1:T(8,128)S(1)}, u32[]{:S(2)}, u32[]{:S(2)}) %all-to-all-start) | async-done | bytes 1835040 | tf_op jit(solution)/shard_map/all_to_all | solution.py:165
  117.7 7.6 %fusion.28 = f32[2,14,64,512,1]{3,2,1,0,4:T(8,128)S(1)} fusion(f32[14,64,512,1]{2,1,0,3:T(8,128)S(1)} %reshape.461, f32[512,1,512]{2,0,1:T(8,128)S(1)} %get-tuple-element.248, f32[512,1,512]{2,0,1:T(8,128)} %get-tuple-element.249), kind=kOutput, calls=%fused_computation.36 | convolution fusion | flops 5637668864 | bytes 7602176 | tf_op jit(solution)/shard_map/aryz,zpk->paryk/dot_general | solution.py:112
  125.3 5.8 fusion.29
  131.1 26.5 %copy.173 = f32[2,14,1,64,512]{1,0,4,3,2:T(2,128)} copy(f32[2,14,1,64,512]{4,3,0,1,2:T(8,128)} %fusion.29) | data formatting | bytes 7340032 | tf_op jit(solution)/shard_map/reshape | solution.py:176
  157.6 56.7 %reshape.479 = f32[32,1,28672]{2,1,0:T(1,128)} reshape(f32[32768,1,2,14]{3,2,1,0:T(2,128)} %bitcast.250) | data formatting | bytes 7340032
  214.3 9.2 %all-to-all-start.1 = ((f32[32,1,28672]{2,1,0:T(1,128)}), f32[32,1,28672]{2,1,0:T(1,128)}, u32[]{:S(2)}, u32[]{:S(2)}) async-start(f32[32,1,28672]{2,1,0:T(1,128)} %reshape.479), calls=%async_computation.1 | async-start | bytes 7340032 | tf_op jit(solution)/shard_map/all_to_all | solution.py:175
  224.6 81.7 %all-to-all-done.1 = f32[32,1,28672]{2,1,0:T(1,128)} async-done(((f32[32,1,28672]{2,1,0:T(1,128)}), f32[32,1,28672]{2,1,0:T(1,128)}, u32[]{:S(2)}, u32[]{:S(2)}) %all-to-all-start.1) | async-done | bytes 3670048 | tf_op jit(solution)/shard_map/all_to_all | solution.py:175
  306.9 12.8 %reduce = f32[32,28672]{1,0:T(8,128)} reduce(f32[32,1,28672]{2,1,0:T(1,128)} %all-to-all-done.1, f32[]{:T(128)} %broadcast.803), dimensions={1}, to_apply=%all_to_all.11.reduce_sub_computation | reduce | bytes 7340036 | tf_op jit(solution)/shard_map/all_to_all | solution.py:175
  319.7 72.2 %reshape.480 = f32[32768,1,2,14]{3,2,1,0:T(2,128)} reshape(f32[32,28672]{1,0:T(8,128)} %reduce) | data formatting | bytes 7340032
  391.9 28.0 %copy.164 = f32[2,14,32,1024,1]{3,2,0,4,1:T(8,128)} copy(f32[2,14,32,1024,1]{1,0,3,2,4:T(2,128)} %bitcast.251) | data formatting | bytes 7340032 | tf_op jit(solution)/shard_map/all_to_all | solution.py:175
  419.9 6.5 convolution_bitcast_fusion
  426.3 85.3 %while.14 = (s32[]{:T(128)}, f32[2,14,32,1024]{3,2,1,0:T(8,128)}, f32[14,14]{0,1:T(8,128)S(1)}, f32[14,14]{0,1:T(8,128)S(1)}, f32[2,14,32,1024]{3,2,0,1:T(8,128)...) while((s32[]{:T(128)}, f32[2,14,32,1024]{3,2,1,0:T(8,128)}, ...), condition=%wide.region_3.4_spmd.clone, body=%wide.region_2.3_spmd.clone.sunk | while | flops 4620291 | bytes 12063295 | solution.py:144
  432.4 4.8 select_add_fusion.2
  438.6 4.8 select_add_fusion.2
  444.8 4.8 select_add_fusion.2
  451.0 4.8 select_add_fusion.2
  457.2 4.8 select_add_fusion.2
  463.4 4.8 select_add_fusion.2
  469.6 4.8 select_add_fusion.2
  475.8 4.8 select_add_fusion.2
  482.0 4.8 select_add_fusion.2
  511.6 6.6 fusion.32
  552.7 78.8 %all-to-all-done.2 = f32[32,2,14,1,1024]{4,1,2,3,0:T(2,128)} async-done(((f32[32,2,14,1,1024]{4,1,2,3,0:T(2,128)}), f32[32,2,14,1,1024]{4,1,2,3,0:T(2,128)}, u32[]{:S(2)}, u32[]{:S(2)}) %all-to-all-start.2) | async-done | bytes 3670048 | tf_op jit(solution)/shard_map/all_to_all | solution.py:19
  631.6 6.0 copy.179
  637.6 5.0 reshape.471
  642.5 6.0 fusion.6
  648.5 7.1 %bitcast_multiply_fusion = f32[14,64,512]{2,1,0:T(8,128)} fusion(f32[1,512,512]{2,1,0:T(8,128)S(1)} %get-tuple-element.254, f32[1,512,512]{2,1,0:T(8,128)S(1)} %get-tuple-element.255, f32[14,512,2,64,1]{1,3,4,2,0:T(8,128)S(1)} %fusion.6), kind=kOutput, calls=%fused_computation.40 | convolution fusion | flops 5638127616 | bytes 7602176 | tf_op jit(solution)/shard_map/paryz,pzk->aryk/dot_general | solution.py:128
  657.7 46.6 %all_to_all.35 = f32[14,1,16,16,128]{4,3,0,1,2:T(8,128)S(1)} all-to-all(f32[14,1,16,16,128]{4,3,0,1,2:T(8,128)S(1)} %bitcast.257), channel_id=1, replica_groups=mesh['gx'=2,'gy'=4,'gz'=4] {'gy','gz'}, dimensions={2} | all-to-all | bytes 3670016 | tf_op jit(solution)/shard_map/all_to_all | solution.py:200
  (144 shorter events, 111.8 us)
Async XLA Ops:
  0.0 64.0 %copy-start = (f32[16,16,128]{2,1,0:T(8,128)S(1)}, f32[16,16,128]{2,1,0:T(8,128)}, u32[]{:S(2)}) copy-start(f32[16,16,128]{2,1,0:T(8,128)} %param.4) | copy-start | bytes 393220
  0.8 3.2 collective-permute-start.1
  2.8 2.6 collective-permute-start
  5.4 4.6 collective-permute-start.2
  9.1 4.4 collective-permute-start.3
  13.7 11.2 %collective-permute-start.4 = (f32[20,20,2]{2,1,0:T(8,128)S(1)}, f32[20,20,2]{2,1,0:T(8,128)S(1)}, u32[]{:S(2)}, u32[]{:S(2)}) collective-permute-start(f32[20,20,2]{2,1,0:T(8,128)S(1)} %get-tuple-element.221), channel_id=1, source_target_pairs={{1,0},{2,1},{3,2},{0,3},{5,4},{6,5},{7,6},{4,7},{9,8},{10,9},{11,1... | collective-permute-start | bytes 9608 | tf_op jit(solution)/shard_map/ppermute | solution.py:32
  17.0 7.9 %collective-permute-start.5 = (f32[20,20,2]{2,1,0:T(8,128)S(1)}, f32[20,20,2]{2,1,0:T(8,128)S(1)}, u32[]{:S(2)}, u32[]{:S(2)}) collective-permute-start(f32[20,20,2]{2,1,0:T(8,128)S(1)} %get-tuple-element.222), channel_id=1, source_target_pairs={{0,1},{1,2},{2,3},{3,0},{4,5},{5,6},{6,7},{7,4},{8,9},{9,10},{10,1... | collective-permute-start | bytes 9608 | tf_op jit(solution)/shard_map/ppermute | solution.py:30
  68.7 44.4 %all-to-all-start = ((f32[14,16,1,16,128]{4,3,0,2,1:T(8,128)}), f32[14,16,1,16,128]{4,3,0,2,1:T(8,128)S(1)}, u32[]{:S(2)}, u32[]{:S(2)}) async-start(f32[14,16,1,16,128]{4,3,0,2,1:T(8,128)} %copy.119), calls=%async_computation | async-start | bytes 3670016 | tf_op jit(solution)/shard_map/all_to_all | solution.py:165
  214.3 9.3 %copy-start.1 = (f32[14,14]{1,0:T(8,128)S(1)}, f32[14,14]{1,0:T(8,128)}, u32[]{:S(2)}) copy-start(f32[14,14]{1,0:T(8,128)} %param.5) | copy-start | bytes 2356
  214.3 92.1 %all-to-all-start.1 = ((f32[32,1,28672]{2,1,0:T(1,128)}), f32[32,1,28672]{2,1,0:T(1,128)}, u32[]{:S(2)}, u32[]{:S(2)}) async-start(f32[32,1,28672]{2,1,0:T(1,128)} %reshape.479), calls=%async_computation.1 | async-start | bytes 7340032 | tf_op jit(solution)/shard_map/all_to_all | solution.py:175
  544.2 87.4 %all-to-all-start.2 = ((f32[32,2,14,1,1024]{4,1,2,3,0:T(2,128)}), f32[32,2,14,1,1024]{4,1,2,3,0:T(2,128)}, u32[]{:S(2)}, u32[]{:S(2)}) async-start(f32[32,2,14,1,1024]{4,1,2,3,0:T(2,128)} %bitcast_dynamic-update-slice_fusion), calls=%async_computation.2 | async-start | bytes 7340032 | tf_op jit(solution)/shard_map/all_to_all | solution.py:19
